TPU v7x, 32 devices: a whole 2x2x4 slice. The times are simulated.
32 devices in a mesh: seq: 8 (over y, x, core), exp: 4 (over z).
Axes of the slice: x: 2, y: 2, z: 4, core: 2. Of those that a mesh axis runs over, the one named last changes fastest.
Arguments:
- queries: bfloat16 [2048, 4096], P('seq', 'exp'), may hold values from -6 to 6
- key_rows: bfloat16 [2048, 512], P('seq'), may hold values from -6 to 6
- value_rows: bfloat16 [2048, 512], P('seq'), may hold values from -6 to 6
- sink_logits: float32 [64], P('exp'), may hold values from -2 to 2
- residual: bfloat16 [2048, 2880], P('seq'), may hold values from -6 to 6
- out_weight: bfloat16 [4096, 2880], P('exp'), may hold values from -0.375 to 0.375
- norm_gain: float32 [2880], replicated, may hold values from 0.25 to 1.75
- expert_ids: int32 [2048, 4], P('seq'), may hold values from 0 to 31, all different within a row; in each aligned block of 256 rows (0 to 255, 256 to 511, ...) at most 48 rows name the same one
- route_gates: float32 [2048, 4], P('seq'), may hold values from 0.1 to 0.6
- gate_proj: bfloat16 [32, 2880, 2048], P('seq', None, 'exp'), may hold values from -0.109375 to 0.109375
- up_proj: bfloat16 [32, 2880, 2048], P('seq', None, 'exp'), may hold values from -0.109375 to 0.109375
- down_proj: bfloat16 [32, 2048, 2880], P('seq', 'exp'), may hold values from -0.125 to 0.125
Outputs:
- layer_out: bfloat16 [2048, 2880], P('seq')
Inputs may be any that keep to these rules, and one draw needn't show every extreme that they name: `expert_ids`: each token names 4 different experts. In each slab of 256 tokens no expert is named by more than 48 entries, and that bound is reached.
All inputs are finite; a program needn't handle non-finite values.
Results may differ from a plain program's by a relative error of at most 0.018.
Values may be sent and summed in bfloat16 or wider, within the bound.
No kernel may reach another device: no remote copies, remote signals or barrier semaphores. Data moves between devices by JAX's collectives and lax.ppermute only.
A program may use at most 128 MiB of HBM per device.

v0:
```python
import math
import jax
import jax.numpy as jnp
from jax import lax
from jax.sharding import PartitionSpec as P

HQ = 64
HK = 8
HEAD = 64
TOP = 4
WIN = 128


def passed_along(x, axis, by):
    count = lax.axis_size(axis)
    pairs = [(i, i + by) for i in range(count) if 0 <= i + by < count]
    return lax.ppermute(x, axis, pairs)


def normalize(mixed, gain):
    wide_vals = mixed.astype(jnp.float32)
    inv_scale = lax.rsqrt(jnp.mean(wide_vals * wide_vals, axis=-1, keepdims=True) + 1e-05)
    return (wide_vals * inv_scale * gain).astype(jnp.bfloat16)


def activate(gate_acc, up_acc):
    gate_acc = jnp.minimum(gate_acc, 7.0)
    up_acc = jnp.clip(up_acc, -7.0, 7.0)
    return ((up_acc + 1.0) * gate_acc * jax.nn.sigmoid(1.702 * gate_acc)).astype(jnp.bfloat16)


def send_back(partial_out):
    return lax.all_to_all(partial_out, "seq", split_axis=0, concat_axis=0, tiled=True)


def on_device(
    queries,
    key_rows,
    value_rows,
    sink_logits,
    residual,
    out_weight,
    norm_gain,
    expert_ids,
    route_gates,
    gate_proj,
    up_proj,
    down_proj,
):
    tok_rows = queries.shape[0]
    local_heads = queries.shape[1] // HEAD
    per_group = HQ // HK
    column = lax.axis_index("exp")
    slab_index = lax.axis_index("seq")
    tail_rows = passed_along((key_rows[tok_rows - WIN :], value_rows[tok_rows - WIN :]), "seq", 1)
    key_full = jnp.concatenate([tail_rows[0], key_rows], 0)
    value_full = jnp.concatenate([tail_rows[1], value_rows], 0)
    kv_count = max(1, local_heads // per_group)
    kv_start = column * local_heads // per_group
    key_sel = lax.dynamic_slice_in_dim(key_full, kv_start * HEAD, kv_count * HEAD, 1).reshape(
        WIN + tok_rows, kv_count, HEAD
    )
    value_sel = lax.dynamic_slice_in_dim(value_full, kv_start * HEAD, kv_count * HEAD, 1).reshape(
        WIN + tok_rows, kv_count, HEAD
    )
    key_heads = jnp.repeat(key_sel, local_heads // kv_count, axis=1)
    value_heads = jnp.repeat(value_sel, local_heads // kv_count, axis=1)
    query_heads = queries.reshape(tok_rows, local_heads, HEAD)
    scores = jnp.einsum(
        "qhd,khd->hqk", query_heads, key_heads, preferred_element_type=jnp.float32
    ) * (1.0 / math.sqrt(HEAD))
    first_pos = slab_index * tok_rows
    q_pos = first_pos + jnp.arange(tok_rows, dtype=jnp.int32)
    k_pos = first_pos - WIN + jnp.arange(WIN + tok_rows, dtype=jnp.int32)
    allowed = (
        (k_pos[None, :] <= q_pos[:, None])
        & (k_pos[None, :] > q_pos[:, None] - WIN)
        & (k_pos[None, :] >= 0)
    )
    scores = jnp.where(allowed[None], scores, -1e30)
    row_top = jnp.maximum(jnp.max(scores, axis=-1), sink_logits[:, None])
    expo = jnp.exp(scores - row_top[..., None])
    denominator = jnp.sum(expo, axis=-1) + jnp.exp(sink_logits[:, None] - row_top)
    weights = (expo / denominator[..., None]).astype(jnp.bfloat16)
    context = jnp.einsum("hqk,khd->qhd", weights, value_heads, preferred_element_type=jnp.float32)
    context = context.astype(jnp.bfloat16).reshape(tok_rows, local_heads * HEAD)
    attn_part = jnp.dot(context, out_weight, preferred_element_type=jnp.float32)
    attn_out = lax.psum(attn_part.astype(jnp.bfloat16), "exp").astype(jnp.float32)
    mixed = (residual.astype(jnp.float32) + attn_out).astype(jnp.bfloat16)
    normed = normalize(mixed, norm_gain)
    local_experts = gate_proj.shape[0]
    seq_count = lax.axis_size("seq")
    experts = local_experts * seq_count
    cap = 3 * tok_rows * TOP // (2 * experts)
    flat_ids = expert_ids.reshape(-1)
    onehot = (flat_ids[:, None] == jnp.arange(experts, dtype=jnp.int32)[None, :]).astype(jnp.int32)
    rank_ids = jnp.cumsum(onehot, axis=0) - 1
    slot_ids = jnp.sum(rank_ids * onehot, axis=1)
    targets = flat_ids * cap + slot_ids
    source = (
        jnp.full((experts * cap,), -1, jnp.int32)
        .at[targets]
        .set(jnp.arange(tok_rows * TOP, dtype=jnp.int32))
    )
    filled = source >= 0
    token_of = jnp.where(filled, source // TOP, 0)
    packed = jnp.where(filled[:, None], normed[token_of], jnp.zeros((), jnp.bfloat16))
    packed = packed.reshape(seq_count, local_experts, cap, packed.shape[1])
    slot_block = lax.all_to_all(packed, "seq", split_axis=0, concat_axis=0, tiled=True)
    gate_acc = jnp.einsum(
        "secd,edf->secf", slot_block, gate_proj, preferred_element_type=jnp.float32
    )
    up_acc = jnp.einsum("secd,edf->secf", slot_block, up_proj, preferred_element_type=jnp.float32)
    hidden = activate(gate_acc, up_acc)
    partial_out = jnp.einsum(
        "secf,efd->secd", hidden, down_proj, preferred_element_type=jnp.float32
    ).astype(jnp.bfloat16)
    returned = send_back(partial_out)
    flat_back = returned.reshape(experts * cap, returned.shape[3])
    picked = flat_back[targets].astype(jnp.float32).reshape(tok_rows, TOP, returned.shape[3])
    moe_part = jnp.sum(picked * route_gates[:, :, None], axis=1)
    moe_total = lax.psum(moe_part.astype(jnp.bfloat16), "exp").astype(jnp.float32)
    return (mixed.astype(jnp.float32) + moe_total).astype(jnp.bfloat16)


def solution(mesh):
    return jax.shard_map(
        on_device,
        mesh=mesh,
        in_specs=(
            P("seq", "exp"),
            P("seq", None),
            P("seq", None),
            P("exp"),
            P("seq", None),
            P("exp", None),
            P(),
            P("seq", None),
            P("seq", None),
            P("seq", None, "exp"),
            P("seq", None, "exp"),
            P("seq", "exp", None),
        ),
        out_specs=P("seq", None),
        check_vma=False,
    )
```

profile of v0, /device:TPU:0, one launch (start us, length us, event | category | flops | bytes accessed | tf_op | source)
XLA Modules:
  0.0 490.9 jit_solution(17000879726990908606)
XLA Ops:
  6.5 1.1 copy.33
  7.7 2.4 collective-permute-start
  10.1 1.1 copy.35
  11.2 4.5 collective-permute-start.1
  15.8 1.2 copy.37
  17.0 0.8 copy.40
  18.3 1.2 fusion.11
  19.6 1.3 fusion.10
  21.1 1.8 fusion.34
  22.9 0.8 slice-done.1
  23.7 2.9 convolution_convert_fusion
  26.7 9.0 %reduce-window.6 = s32[32,8,128]{2,1,0:T(8,128)S(1)} reduce-window(s32[32,8,128]{2,1,0:T(8,128)S(1)} %fusion.37, s32[]{:T(128)} %constant.27.clone.1), window={size=1x1x128 pad=0_0x0_0x127_0}, to_apply=%region_3.4 | reduce-window | flops 4161536 | bytes 262148 | tf_op jit(solution)/shard_map/reduce-window
  36.5 4.5 scatter_custom_fusion
  41.2 52.9 %all-reduce.3.cloned.1.call-done = bf16[256,2880]{0,1:T(8,128)(2,1)} async-done(((bf16[256,2880]{0,1:T(8,128)(2,1)}), bf16[256,2880]{0,1:T(8,128)(2,1)}) %all-reduce.3.cloned.1.call-update) | async-done | bytes 1474576 | tf_op jit(solution)/shard_map/psum | solution.py:88
  94.1 1.9 fusion.13
  96.0 3.0 fusion.15
  99.1 1.8 copy.44
  100.9 8.1 %gather_fusion = bf16[1536,2880]{1,0:T(8,128)(2,1)} fusion(bf16[256,2880]{1,0:T(8,128)(2,1)S(1)} %copy.44, s32[2048]{0:T(1024)S(1)} %pad_clamp_fusion), kind=kCustom, calls=%fused_computation | custom fusion | bytes 17700864 | tf_op jit(solution)/shard_map/gather | solution.py:107
  109.0 8.0 %broadcast_select_fusion = bf16[8,4,48,2880]{3,2,1,0:T(8,128)(2,1)} fusion(bf16[8,4,48,2880]{3,2,1,0:T(8,128)(2,1)} %bitcast.70, pred[8,4,48]{2,1,0:T(4,128)(4,1)S(1)} %broadcast_in_dim.62), kind=kLoop, calls=%fused_computation.11 | loop fusion | flops 4423680 | bytes 17696256 | tf_op jit(solution)/shard_map/jit(_where)/select_n | solution.py:107
  117.0 104.8 %all_to_all.10 = bf16[8,4,48,2880]{3,2,1,0:T(8,128)(2,1)S(1)} all-to-all(bf16[8,4,48,2880]{3,2,1,0:T(8,128)(2,1)} %broadcast_select_fusion), channel_id=1, replica_groups=mesh['seq'=8,'exp'=4] {'seq'}, dimensions={0} | all-to-all | bytes 17694720 | tf_op jit(solution)/shard_map/all_to_all | solution.py:109
  221.8 3.5 copy-done.2
  225.3 9.6 %fusion.2 = f32[4,8,48,512]{3,2,1,0:T(8,128)} fusion(bf16[4,2880,512]{2,1,0:T(8,128)(2,1)} %param.21, bf16[8,4,48,2880]{3,2,1,0:T(8,128)(2,1)S(1)} %all_to_all.10), kind=kOutput, calls=%fused_computation.6 | convolution fusion | flops 4529848320 | bytes 23789568 | tf_op jit(solution)/shard_map/secd,edf->secf/dot_general | solution.py:110
  235.0 25.9 %convert_bitcast_fusion = bf16[8,4,48,2880]{3,2,0,1:T(8,128)(2,1)} fusion(bf16[4,512,2880]{1,2,0:T(8,128)(2,1)} %param.23, f32[4,8,48,512]{3,2,1,0:T(8,128)} %fusion.2, bf16[4,2880,512]{2,1,0:T(8,128)(2,1)} %param.22, bf16[8,4,48,2880]{3,2,1,0:T(8,128)(2,1)} %copy-done.2), kind=kOutput, calls=%fused_computation.10 | convolution fusion | flops 9071984640 | bytes 44433408 | tf_op jit(solution)/shard_map/secf,efd->secd/dot_general | solution.py:115
  260.8 7.9 %copy.47 = bf16[8,4,48,2880]{3,2,1,0:T(8,128)(2,1)} copy(bf16[8,4,48,2880]{3,2,0,1:T(8,128)(2,1)} %convert_bitcast_fusion) | data formatting | bytes 17694720 | tf_op jit(solution)/shard_map/convert_element_type | solution.py:117
  268.7 5.1 %all-to-all-start.1 = ((bf16[8,4,48,2880]{3,2,1,0:T(8,128)(2,1)}), bf16[8,4,48,2880]{3,2,1,0:T(8,128)(2,1)}, u32[]{:S(2)}, u32[]{:S(2)}) async-start(bf16[8,4,48,2880]{3,2,1,0:T(8,128)(2,1)} %copy.47), calls=%async_computation.1 | async-start | bytes 18087936 | tf_op jit(solution)/shard_map/all_to_all | solution.py:33
  274.3 100.6 %all-to-all-done.1 = bf16[8,4,48,2880]{3,2,1,0:T(8,128)(2,1)} async-done(((bf16[8,4,48,2880]{3,2,1,0:T(8,128)(2,1)}), bf16[8,4,48,2880]{3,2,1,0:T(8,128)(2,1)}, u32[]{:S(2)}, u32[]{:S(2)}) %all-to-all-start.1) | async-done | bytes 8847392 | tf_op jit(solution)/shard_map/all_to_all | solution.py:33
  374.9 16.4 %gather_fusion.1 = bf16[1024,2880]{1,0:T(8,128)(2,1)} fusion(bf16[1536,2880]{1,0:T(8,128)(2,1)} %bitcast.21, s32[1024]{0:T(1024)S(1)} %broadcast_clamp_fusion), kind=kCustom, calls=%fused_computation.1 | custom fusion | bytes 11800576 | tf_op jit(solution)/shard_map/gather | solution.py:120
  391.3 11.7 %reshape.236 = f32[256,4,2880]{2,1,0:T(4,128)} reshape(bf16[1024,2880]{1,0:T(8,128)(2,1)} %gather_fusion.1) | data formatting | bytes 17694720 | tf_op jit(solution)/shard_map/convert_element_type | solution.py:120
  403.0 12.1 %multiply_reduce_fusion = bf16[256,2880]{1,0:T(8,128)(2,1)} fusion(f32[256,4,2880]{2,1,0:T(4,128)} %reshape.236, f32[256,4]{1,0:T(8,128)S(1)} %copy.48), kind=kLoop, calls=%fused_computation.3 | loop fusion | flops 5160960 | bytes 13275136 | tf_op jit(solution)/shard_map/reduce_sum | solution.py:121
  415.1 2.5 copy.49
  417.7 63.3 %all-reduce.5.cloned.1.call-done = bf16[256,2880]{0,1:T(8,128)(2,1)} async-done(((bf16[256,2880]{0,1:T(8,128)(2,1)}), bf16[256,2880]{0,1:T(8,128)(2,1)}) %all-reduce.5.cloned.1.call-update) | async-done | bytes 1474576 | tf_op jit(solution)/shard_map/psum | solution.py:122
  481.0 3.0 fusion.16
  (56 shorter events, 2.2 us)
Async XLA Ops:
  6.5 87.5 %all-reduce.3.cloned.1.call-start = ((), (), s32[]{:S(2)}) async-start(), calls=%async_computation.2 | async-start | bytes 2949120 | tf_op jit(solution)/shard_map/psum | solution.py:88
  7.6 11.8 %copy-start.6 = (f32[16]{0:T(128)S(1)}, f32[16]{0:T(128)}, u32[]{:S(2)}) copy-start(f32[16]{0:T(128)} %param.15) | copy-start | bytes 196
  7.7 10.5 %collective-permute-start = (bf16[128,512]{0,1:T(8,128)(2,1)S(1)}, bf16[128,512]{0,1:T(8,128)(2,1)S(1)}, u32[]{:S(2)}, u32[]{:S(2)}) collective-permute-start(bf16[128,512]{0,1:T(8,128)(2,1)S(1)} %slice.20), channel_id=1, source_target_pairs={{0,4},{4,8},{8,12},{12,16},{16,20},{20,24},{24,28},{1,5},{5,9},{9,... | collective-permute-start | bytes 393224 | tf_op jit(solution)/shard_map/ppermute | solution.py:17
  11.2 7.0 %collective-permute-start.1 = (bf16[128,512]{0,1:T(8,128)(2,1)S(1)}, bf16[128,512]{0,1:T(8,128)(2,1)S(1)}, u32[]{:S(2)}, u32[]{:S(2)}) collective-permute-start(bf16[128,512]{0,1:T(8,128)(2,1)S(1)} %slice.21), channel_id=1, source_target_pairs={{0,4},{4,8},{8,12},{12,16},{16,20},{20,24},{24,28},{1,5},{5,9},{9,... | collective-permute-start | bytes 393224 | tf_op jit(solution)/shard_map/ppermute | solution.py:17
  20.9 2.0 slice-start
  21.0 2.6 slice-start.1
  23.7 12.4 %copy-start.3 = (s32[256,4]{0,1:T(4,128)S(1)}, s32[256,4]{0,1:T(4,128)}, u32[]{:S(2)}) copy-start(s32[256,4]{0,1:T(4,128)} %param.19) | copy-start | bytes 12292
  23.7 70.4 %copy-start = (bf16[256,2880]{0,1:T(8,128)(2,1)S(1)}, bf16[256,2880]{0,1:T(8,128)(2,1)}, u32[]{:S(2)}) copy-start(bf16[256,2880]{0,1:T(8,128)(2,1)} %param.16) | copy-start | bytes 4423684
  26.5 69.5 %copy-start.4 = (f32[2880]{0:T(1024)S(1)}, f32[2880]{0:T(1024)}, u32[]{:S(2)}) copy-start(f32[2880]{0:T(1024)} %param.18) | copy-start | bytes 34564
  221.8 3.5 copy-start.2
  268.7 5.4 %copy-start.5 = (f32[256,4]{0,1:T(4,128)S(1)}, f32[256,4]{0,1:T(4,128)}, u32[]{:S(2)}) copy-start(f32[256,4]{0,1:T(4,128)} %param.20) | copy-start | bytes 12292
  268.7 106.2 %all-to-all-start.1 = ((bf16[8,4,48,2880]{3,2,1,0:T(8,128)(2,1)}), bf16[8,4,48,2880]{3,2,1,0:T(8,128)(2,1)}, u32[]{:S(2)}, u32[]{:S(2)}) async-start(bf16[8,4,48,2880]{3,2,1,0:T(8,128)(2,1)} %copy.47), calls=%async_computation.1 | async-start | bytes 18087936 | tf_op jit(solution)/shard_map/all_to_all | solution.py:33
  273.8 207.2 %all-reduce.5.cloned.1.call-start = ((), (), s32[]{:S(2)}) async-start(), calls=%async_computation.3 | async-start | bytes 2949120 | tf_op jit(solution)/shard_map/psum | solution.py:122
  403.0 78.0 %copy-start.1 = (bf16[256,2880]{0,1:T(8,128)(2,1)S(1)}, bf16[256,2880]{0,1:T(8,128)(2,1)}, u32[]{:S(2)}) copy-start(bf16[256,2880]{0,1:T(8,128)(2,1)} %all-reduce.3.cloned.1.call-done) | copy-start | bytes 4423684
Sparse Core Ops, SparseCore 0:
  26.7 67.3 all-reduce.2
  417.8 63.1 all-reduce.4
where the time goes:
time: 492 us; the launch traced here: 491 us
  waiting for transfers between devices  217 us (44%)
  blocking collectives  105 us (21%)
  local copies, waits for them, and re-layouts  62.8 us (13%)
  matrix products  41.4 us (8%)
  other arithmetic  39 us (8%)
  between operations  13.8 us (3%)
  starting transfers between devices  12.3 us (2%)
    all_to_all x1, blocking collectives, on_device(): lax.all_to_all(packed, 'seq', split_axis=0, concat_axis=0, tiled=True)  105 us
    all_to_all x1, waiting for transfers between devices, send_back(): lax.all_to_all(partial_out, 'seq', split_axis=0, concat_axis=0, tiled=True)  101 us
    psum x1, waiting for transfers between devices, on_device(): lax.psum(moe_part.astype(jnp.bfloat16), 'exp').astype(jnp.float32)  63.3 us
    psum x1, waiting for transfers between devices, on_device(): lax.psum(attn_part.astype(jnp.bfloat16), 'exp').astype(jnp.float32)  52.9 us
    dot_general x1, matrix products, on_device(): jnp.einsum('secf,efd->secd', hidden, down_proj, preferred_element_type=jn...  25.9 us
    gather x1, local copies, waits for them, and re-layouts, on_device(): flat_back[targets].astype(jnp.float32)  16.4 us
    reduce_sum x1, other arithmetic, on_device(): moe_part = jnp.sum(picked * route_gates[:, :, None], axis=1)  12.1 us
    convert_element_type x1, local copies, waits for them, and re-layouts, on_device(): flat_back[targets].astype(jnp.float32)  11.7 us
  transfers between devices with their start and end apart: 5, of which 3 were waited for; matrix products, arithmetic and copies ran while one was open for 4% of the time, Pallas kernels for 0%

commit v1 on v0

--- a/solution.py
+++ b/solution.py
@@ -9,6 +9,12 @@
 HEAD = 64
 TOP = 4
 WIN = 128
+
+
+def gather_and_add(x, mesh_axis):
+    parts = lax.all_gather(x, mesh_axis, axis=0, tiled=False)
+    total = parts.sum(axis=0)
+    return total
 
 
 def passed_along(x, axis, by):
@@ -85,7 +91,7 @@
     context = jnp.einsum("hqk,khd->qhd", weights, value_heads, preferred_element_type=jnp.float32)
     context = context.astype(jnp.bfloat16).reshape(tok_rows, local_heads * HEAD)
     attn_part = jnp.dot(context, out_weight, preferred_element_type=jnp.float32)
-    attn_out = lax.psum(attn_part.astype(jnp.bfloat16), "exp").astype(jnp.float32)
+    attn_out = gather_and_add(attn_part.astype(jnp.bfloat16), "exp").astype(jnp.float32)
     mixed = (residual.astype(jnp.float32) + attn_out).astype(jnp.bfloat16)
     normed = normalize(mixed, norm_gain)
     local_experts = gate_proj.shape[0]

time: 492 us -> 559 us (1.14)
  waiting for transfers between devices: 217 us -> 261 us
  other arithmetic: 39 us -> 51.5 us
  local copies, waits for them, and re-layouts: 62.8 us -> 73.7 us
    all_gather x0 -> x1, waiting for transfers between devices: none -> 96.2 us  [gather_and_add(): parts = lax.all_gather(x, mesh_axis, axis=0, tiled=False)]
    psum x1 -> x0, waiting for transfers between devices: 52.9 us -> none  [on_device(): lax.psum(attn_part.astype(jnp.bfloat16), 'exp').astype(jnp.float32)]
    reduce_sum x0 -> x1, other arithmetic: none -> 15.3 us  [gather_and_add(): total = parts.sum(axis=0)]
    all_gather x0 -> x1, local copies, waits for them, and re-layouts: none -> 11.6 us  [gather_and_add(): parts = lax.all_gather(x, mesh_axis, axis=0, tiled=False)]
  transfers between devices with their start and end apart: 5 -> 5, of which waited for: 3 -> 3; matrix products, arithmetic and copies ran while one was open for 4% -> 3% of each run, Pallas kernels for 0% -> 0%
where the time goes in v1:
time: 559 us; the launch traced here: 558 us
  waiting for transfers between devices  261 us (47%)
  blocking collectives  105 us (19%)
  local copies, waits for them, and re-layouts  73.7 us (13%)
  other arithmetic  51.5 us (9%)
  matrix products  41.4 us (7%)
  between operations  13.8 us (2%)
  starting transfers between devices  12.3 us (2%)
    all_to_all x1, blocking collectives, on_device(): lax.all_to_all(packed, 'seq', split_axis=0, concat_axis=0, tiled=True)  105 us
    all_to_all x1, waiting for transfers between devices, send_back(): lax.all_to_all(partial_out, 'seq', split_axis=0, concat_axis=0, tiled=True)  101 us
    all_gather x1, waiting for transfers between devices, gather_and_add(): parts = lax.all_gather(x, mesh_axis, axis=0, tiled=False)  96.2 us
    psum x1, waiting for transfers between devices, on_device(): lax.psum(moe_part.astype(jnp.bfloat16), 'exp').astype(jnp.float32)  63.8 us
    dot_general x1, matrix products, on_device(): jnp.einsum('secf,efd->secd', hidden, down_proj, preferred_element_type=jn...  25.9 us
    gather x1, local copies, waits for them, and re-layouts, on_device(): flat_back[targets].astype(jnp.float32)  16.4 us
    reduce_sum x1, other arithmetic, gather_and_add(): total = parts.sum(axis=0)  15.3 us
    reduce_sum x1, other arithmetic, on_device(): moe_part = jnp.sum(picked * route_gates[:, :, None], axis=1)  12.1 us
  transfers between devices with their start and end apart: 5, of which 3 were waited for; matrix products, arithmetic and copies ran while one was open for 3% of the time, Pallas kernels for 0%

profile of v1, /device:TPU:0, one launch (start us, length us, event | category | flops | bytes accessed | tf_op | source)
XLA Modules:
  0.0 558.1 jit_solution(9907871279645754166)
XLA Ops:
  6.5 1.1 copy.69
  7.7 2.4 collective-permute-start
  10.1 1.1 copy.71
  11.2 4.5 collective-permute-start.1
  15.8 1.2 copy.73
  17.4 1.2 fusion.11
  18.6 1.3 fusion.10
  20.1 1.8 fusion.34
  22.7 2.9 convolution_convert_fusion
  26.0 9.0 %reduce-window.6 = s32[32,8,128]{2,1,0:T(8,128)S(1)} reduce-window(s32[32,8,128]{2,1,0:T(8,128)S(1)} %fusion.37, s32[]{:T(128)} %constant.27.clone.1), window={size=1x1x128 pad=0_0x0_0x127_0}, to_apply=%region_3.4 | reduce-window | flops 4161536 | bytes 262148 | tf_op jit(solution)/shard_map/reduce-window
  35.9 4.5 scatter_custom_fusion
  40.5 96.2 %all-gather.3.cloned.1.call-done = bf16[1024,2880]{0,1:T(8,128)(2,1)} async-done(((bf16[256,2880]{0,1:T(8,128)(2,1)}), bf16[1024,2880]{0,1:T(8,128)(2,1)}) %all-gather.3.cloned.1.call-update) | async-done | bytes 5898256 | tf_op jit(solution)/shard_map/all_gather | solution.py:15
  136.7 11.6 %reshape.261 = bf16[4,256,2880]{1,0,2:T(4,128)(2,1)} reshape(bf16[1024,2880]{0,1:T(8,128)(2,1)} %all-gather.3.cloned.1.call-done) | data formatting | bytes 11796480 | tf_op jit(solution)/shard_map/all_gather | solution.py:15
  148.3 15.3 %reduce_sum.51 = bf16[256,2880]{0,1:T(8,128)(2,1)S(1)} reduce(bf16[4,256,2880]{1,0,2:T(4,128)(2,1)} %reshape.261, bf16[]{:T(256)} %constant.81.clone.1), dimensions={0}, to_apply=%region_2.3 | reduce | flops 2211840 | bytes 7372802 | tf_op jit(solution)/shard_map/reduce_sum | solution.py:16
  163.6 0.6 fusion.13
  164.2 1.7 fusion.15
  165.8 1.8 copy.80
  167.7 8.1 %gather_fusion = bf16[1536,2880]{1,0:T(8,128)(2,1)} fusion(bf16[256,2880]{1,0:T(8,128)(2,1)S(1)} %copy.80, s32[2048]{0:T(1024)S(1)} %pad_clamp_fusion), kind=kCustom, calls=%fused_computation | custom fusion | bytes 17700864 | tf_op jit(solution)/shard_map/gather | solution.py:113
  175.8 8.0 %broadcast_select_fusion = bf16[8,4,48,2880]{3,2,1,0:T(8,128)(2,1)} fusion(bf16[8,4,48,2880]{3,2,1,0:T(8,128)(2,1)} %bitcast.72, pred[8,4,48]{2,1,0:T(4,128)(4,1)S(1)} %broadcast_in_dim.62), kind=kLoop, calls=%fused_computation.11 | loop fusion | flops 4423680 | bytes 17696256 | tf_op jit(solution)/shard_map/jit(_where)/select_n | solution.py:113
  183.8 104.8 %all_to_all.10 = bf16[8,4,48,2880]{3,2,1,0:T(8,128)(2,1)S(1)} all-to-all(bf16[8,4,48,2880]{3,2,1,0:T(8,128)(2,1)} %broadcast_select_fusion), channel_id=1, replica_groups=mesh['seq'=8,'exp'=4] {'seq'}, dimensions={0} | all-to-all | bytes 17694720 | tf_op jit(solution)/shard_map/all_to_all | solution.py:115
  288.6 3.5 copy-done.2
  292.1 9.6 %fusion.2 = f32[4,8,48,512]{3,2,1,0:T(8,128)} fusion(bf16[4,2880,512]{2,1,0:T(8,128)(2,1)} %param.21, bf16[8,4,48,2880]{3,2,1,0:T(8,128)(2,1)S(1)} %all_to_all.10), kind=kOutput, calls=%fused_computation.6 | convolution fusion | flops 4529848320 | bytes 23789568 | tf_op jit(solution)/shard_map/secd,edf->secf/dot_general | solution.py:116
  301.8 25.9 %convert_bitcast_fusion = bf16[8,4,48,2880]{3,2,0,1:T(8,128)(2,1)} fusion(bf16[4,512,2880]{1,2,0:T(8,128)(2,1)} %param.23, f32[4,8,48,512]{3,2,1,0:T(8,128)} %fusion.2, bf16[4,2880,512]{2,1,0:T(8,128)(2,1)} %param.22, bf16[8,4,48,2880]{3,2,1,0:T(8,128)(2,1)} %copy-done.2), kind=kOutput, calls=%fused_computation.10 | convolution fusion | flops 9071984640 | bytes 44433408 | tf_op jit(solution)/shard_map/secf,efd->secd/dot_general | solution.py:121
  327.6 7.9 %copy.83 = bf16[8,4,48,2880]{3,2,1,0:T(8,128)(2,1)} copy(bf16[8,4,48,2880]{3,2,0,1:T(8,128)(2,1)} %convert_bitcast_fusion) | data formatting | bytes 17694720 | tf_op jit(solution)/shard_map/convert_element_type | solution.py:123
  335.5 5.3 all-to-all-start.1
  341.1 100.6 %all-to-all-done.1 = bf16[8,4,48,2880]{3,2,1,0:T(8,128)(2,1)} async-done(((bf16[8,4,48,2880]{3,2,1,0:T(8,128)(2,1)}), bf16[8,4,48,2880]{3,2,1,0:T(8,128)(2,1)}, u32[]{:S(2)}, u32[]{:S(2)}) %all-to-all-start.1) | async-done | bytes 8847392 | tf_op jit(solution)/shard_map/all_to_all | solution.py:39
  441.7 16.4 %gather_fusion.1 = bf16[1024,2880]{1,0:T(8,128)(2,1)} fusion(bf16[1536,2880]{1,0:T(8,128)(2,1)} %bitcast.21, s32[1024]{0:T(1024)S(1)} %broadcast_clamp_fusion), kind=kCustom, calls=%fused_computation.1 | custom fusion | bytes 11800576 | tf_op jit(solution)/shard_map/gather | solution.py:126
  458.1 11.7 %reshape.236 = f32[256,4,2880]{2,1,0:T(4,128)} reshape(bf16[1024,2880]{1,0:T(8,128)(2,1)} %gather_fusion.1) | data formatting | bytes 17694720 | tf_op jit(solution)/shard_map/convert_element_type | solution.py:126
  469.8 12.1 %multiply_reduce_fusion = bf16[256,2880]{1,0:T(8,128)(2,1)} fusion(f32[256,4,2880]{2,1,0:T(4,128)} %reshape.236, f32[256,4]{1,0:T(8,128)S(1)} %copy.84), kind=kLoop, calls=%fused_computation.3 | loop fusion | flops 5160960 | bytes 13275136 | tf_op jit(solution)/shard_map/reduce_sum | solution.py:127
  481.9 2.5 copy.85
  484.5 63.8 %all-reduce.2.cloned.1.call-done = bf16[256,2880]{0,1:T(8,128)(2,1)} async-done(((bf16[256,2880]{0,1:T(8,128)(2,1)}), bf16[256,2880]{0,1:T(8,128)(2,1)}) %all-reduce.2.cloned.1.call-update) | async-done | bytes 1474576 | tf_op jit(solution)/shard_map/psum | solution.py:128
  548.2 3.0 fusion.16
  (58 shorter events, 2.9 us)
Async XLA Ops:
  6.5 130.1 %all-gather.3.cloned.1.call-start = ((), (), s32[]{:S(2)}) async-start(), calls=%async_computation.3 | async-start | bytes 7372800 | tf_op jit(solution)/shard_map/all_gather | solution.py:15
  7.6 10.9 %copy-start.6 = (f32[16]{0:T(128)S(1)}, f32[16]{0:T(128)}, u32[]{:S(2)}) copy-start(f32[16]{0:T(128)} %param.15) | copy-start | bytes 196
  7.7 9.5 %collective-permute-start = (bf16[128,512]{0,1:T(8,128)(2,1)S(1)}, bf16[128,512]{0,1:T(8,128)(2,1)S(1)}, u32[]{:S(2)}, u32[]{:S(2)}) collective-permute-start(bf16[128,512]{0,1:T(8,128)(2,1)S(1)} %slice.20), channel_id=1, source_target_pairs={{0,4},{4,8},{8,12},{12,16},{16,20},{20,24},{24,28},{1,5},{5,9},{9,... | collective-permute-start | bytes 393224 | tf_op jit(solution)/shard_map/ppermute | solution.py:23
  11.2 6.0 %collective-permute-start.1 = (bf16[128,512]{0,1:T(8,128)(2,1)S(1)}, bf16[128,512]{0,1:T(8,128)(2,1)S(1)}, u32[]{:S(2)}, u32[]{:S(2)}) collective-permute-start(bf16[128,512]{0,1:T(8,128)(2,1)S(1)} %slice.21), channel_id=1, source_target_pairs={{0,4},{4,8},{8,12},{12,16},{16,20},{20,24},{24,28},{1,5},{5,9},{9,... | collective-permute-start | bytes 393224 | tf_op jit(solution)/shard_map/ppermute | solution.py:23
  20.0 2.2 slice-start
  20.1 2.6 slice-start.1
  22.7 2.9 copy-start.3
  148.3 15.3 %copy-start = (bf16[256,2880]{0,1:T(8,128)(2,1)S(1)}, bf16[256,2880]{0,1:T(8,128)(2,1)}, u32[]{:S(2)}) copy-start(bf16[256,2880]{0,1:T(8,128)(2,1)} %param.16) | copy-start | bytes 4423684
  148.3 15.9 %copy-start.4 = (f32[2880]{0:T(1024)S(1)}, f32[2880]{0:T(1024)}, u32[]{:S(2)}) copy-start(f32[2880]{0:T(1024)} %param.18) | copy-start | bytes 34564
  288.6 3.5 copy-start.2
  335.5 5.4 copy-start.5
  335.5 106.2 %all-to-all-start.1 = ((bf16[8,4,48,2880]{3,2,1,0:T(8,128)(2,1)}), bf16[8,4,48,2880]{3,2,1,0:T(8,128)(2,1)}, u32[]{:S(2)}, u32[]{:S(2)}) async-start(bf16[8,4,48,2880]{3,2,1,0:T(8,128)(2,1)} %copy.83), calls=%async_computation.1 | async-start | bytes 18087936 | tf_op jit(solution)/shard_map/all_to_all | solution.py:39
  340.9 207.4 %all-reduce.2.cloned.1.call-start = ((), (), s32[]{:S(2)}) async-start(), calls=%async_computation.2 | async-start | bytes 2949120 | tf_op jit(solution)/shard_map/psum | solution.py:128
  469.8 78.4 %copy-start.1 = (bf16[256,2880]{0,1:T(8,128)(2,1)S(1)}, bf16[256,2880]{0,1:T(8,128)(2,1)}, u32[]{:S(2)}) copy-start(bf16[256,2880]{0,1:T(8,128)(2,1)} %param.16) | copy-start | bytes 4423684
Sparse Core Ops, SparseCore 0:
  25.7 110.8 all-gather.2
  484.6 63.6 all-reduce.1
